TPU v7x, 32 devices: a whole 2x2x4 slice. The times are simulated.
32 devices in a mesh: pool: 2 (over y), blk: 4 (over x, core), batch: 4 (over z).
Axes of the slice: x: 2, y: 2, z: 4, core: 2. Of those that a mesh axis runs over, the one named last changes fastest.
Arguments:
- prompt: bfloat16 [8, 512, 4096], P(('pool', 'batch'), 'blk'), may hold values from -40 to 40
- prompt_len: int32 [2, 4], P('pool', 'batch'), may hold values from 128 to 512
- dec_tokens: bfloat16 [4, 32, 4096], P(None, ('pool', 'batch')), may hold values from -40 to 40
- cache_k: bfloat16 [32, 4096, 1024], P(('pool', 'batch'), None, 'blk'), may hold values from -72 to 72
- cache_v: bfloat16 [32, 4096, 1024], P(('pool', 'batch'), None, 'blk'), may hold values from -6 to 6
- cache_len: int32 [32], P(('pool', 'batch')), may hold values from 1 to 4092
- assign: int32 [2, 4], P('pool', 'batch'), may hold values from 0 to 3, each once within a row
- slot: int32 [2, 4], P('pool', 'batch'), may hold values from 0 to 3
- gain: float32 [4096], replicated, may hold values from 0.5 to 1.5
- w_qkv: bfloat16 [4096, 6144], P(None, 'blk'), may hold values from -4 to 4
- w_out: bfloat16 [4096, 4096], P('blk'), may hold values from -0.09375 to 0.09375
Outputs:
- prefill_out: bfloat16 [8, 512, 4096], P(('pool', 'batch'), 'blk')
- dec_out: bfloat16 [4, 32, 4096], P(None, ('pool', 'batch'))
Inputs may be any that keep to these rules, and one draw needn't show every extreme that they name: For each pool p, assign[p] is a permutation of the 4 stretch indices of the other pool.
All inputs are finite; a program needn't handle non-finite values.
Results may differ from a plain program's by a relative error of at most 0.011.
Values may be sent and summed in bfloat16 or wider, within the bound.
No kernel may reach another device: no remote copies, remote signals or barrier semaphores. Data moves between devices by JAX's collectives and lax.ppermute only.
A program may use at most 128 MiB of HBM per device.

v0:
```python
import jax
import jax.numpy as jnp
from jax import lax
from jax.sharding import PartitionSpec as P

HEAD_DIM = 128
GROUP = 4
EPSILON = 1e-05
THETA = 500000.0


def rms_norm(values, gain):
    wide = values.astype(jnp.float32)
    factor = lax.rsqrt(jnp.mean(wide * wide, axis=-1, keepdims=True) + EPSILON)
    return (wide * factor * gain).astype(jnp.bfloat16)


def rotate(vector, places):
    half = vector.shape[-1] // 2
    freqs = THETA ** (-jnp.arange(half, dtype=jnp.float32) / half)
    angles = places.astype(jnp.float32)[..., None] * freqs
    cosine = jnp.cos(angles)
    sine = jnp.sin(angles)
    first = vector[..., :half]
    second = vector[..., half:]
    return jnp.concatenate(
        [first * cosine - second * sine, second * cosine + first * sine], axis=-1
    )


def softmax_weights(scores):
    top = jnp.max(scores, axis=-1, keepdims=True)
    expo = jnp.exp(scores - top)
    return (expo / jnp.sum(expo, axis=-1, keepdims=True)).astype(jnp.bfloat16)


def make_picker(wanted, carry, piece):
    count = piece[0].shape[0]
    match = jnp.arange(count, dtype=jnp.int32) == wanted
    keys = jnp.sum(jnp.where(match[:, None, None], piece[0].astype(jnp.float32), 0.0), axis=0)
    values = jnp.sum(jnp.where(match[:, None, None], piece[1].astype(jnp.float32), 0.0), axis=0)
    length = carry[2] + jnp.sum(jnp.where(match, piece[2], 0))
    return (keys, values, length)


def attend(
    query,
    cache_key,
    cache_value,
    lengths,
    fresh,
    new_key,
    new_value,
    new_len,
    own_key,
    own_value,
    own_mask,
):
    f32 = jnp.float32
    scale = query.shape[-1] ** (-0.5)
    old = jnp.einsum("srhgd,rchd->srhgc", query, cache_key, preferred_element_type=f32) * scale
    span = jnp.arange(cache_key.shape[1], dtype=jnp.int32)
    old_ok = (span[None, :] < lengths[:, None]) & jnp.logical_not(fresh)[:, None]
    old = jnp.where(old_ok[None, :, None, None, :], old, -jnp.inf)
    new = jnp.einsum("srhgd,chd->srhgc", query, new_key, preferred_element_type=f32) * scale
    reach = jnp.arange(new_key.shape[0], dtype=jnp.int32)
    new_ok = (reach[None, :] < new_len) & fresh[:, None]
    new = jnp.where(new_ok[None, :, None, None, :], new, -jnp.inf)
    own = jnp.einsum("srhgd,trhd->srhgt", query, own_key, preferred_element_type=f32) * scale
    own = jnp.where(own_mask[:, None, None, None, :], own, -jnp.inf)
    cached = cache_key.shape[1]
    fresh_count = new_key.shape[0]
    probs = softmax_weights(jnp.concatenate([old, new, own], axis=-1))
    mixed = jnp.einsum(
        "srhgc,rchd->srhgd", probs[..., :cached], cache_value, preferred_element_type=f32
    )
    mixed = mixed + jnp.einsum(
        "srhgc,chd->srhgd",
        probs[..., cached : cached + fresh_count],
        new_value,
        preferred_element_type=f32,
    )
    mixed = mixed + jnp.einsum(
        "srhgt,trhd->srhgd",
        probs[..., cached + fresh_count :],
        own_value,
        preferred_element_type=f32,
    )
    return mixed.astype(jnp.bfloat16)


def body(
    prompt, prompt_len, dec_tokens, cache_k, cache_v, cache_len, assign, slot, gain, w_qkv, w_out
):
    f32 = jnp.float32
    bf16 = jnp.bfloat16
    local = w_out.shape[0] // (GROUP * HEAD_DIM)
    scale = HEAD_DIM ** (-0.5)
    normed = rms_norm(prompt[0], gain)
    joined = jnp.dot(
        lax.all_gather(normed, "blk", axis=0, tiled=True), w_qkv, preferred_element_type=f32
    )
    stretch = joined.shape[0]
    joined = joined.reshape(stretch, local, GROUP + 2, HEAD_DIM)
    places = jnp.arange(stretch, dtype=jnp.int32)
    query = rotate(joined[:, :, :GROUP], places[:, None, None]).astype(bf16)
    key = rotate(joined[:, :, GROUP], places[:, None]).astype(bf16)
    value = joined[:, :, GROUP + 1].astype(bf16)
    plen = prompt_len[0, 0]
    scores = jnp.einsum("qhgd,khd->hgqk", query, key, preferred_element_type=f32) * scale
    allowed = (places[None, :] <= places[:, None]) & (places[None, :] < plen)
    scores = jnp.where(allowed, scores, -jnp.inf)
    probs = softmax_weights(scores)
    mixed = jnp.einsum("hgqk,khd->qhgd", probs, value, preferred_element_type=f32).astype(bf16)
    mixed = mixed.reshape(stretch, local * GROUP * HEAD_DIM)
    rows = mixed
    summed = lax.psum_scatter(
        jnp.dot(rows, w_out, preferred_element_type=f32).astype(jnp.bfloat16),
        "blk",
        scatter_dimension=0,
        tiled=True,
    ).astype(jnp.float32)
    prefill_out = (prompt[0].astype(f32) + summed).astype(bf16)[None]
    packet = (
        key.reshape(1, stretch, local * HEAD_DIM),
        value.reshape(1, stretch, local * HEAD_DIM),
        prompt_len.reshape(1),
    )
    empty = (
        jnp.zeros((stretch, local * HEAD_DIM), f32),
        jnp.zeros((stretch, local * HEAD_DIM), f32),
        jnp.zeros((), jnp.int32),
    )
    wanted = assign[0, 0]
    source = (1 - lax.axis_index("pool")) * lax.axis_size("batch") + wanted
    arrived = make_picker(
        source,
        empty,
        (
            lax.all_gather(packet[0], ("pool", "batch"), axis=0, tiled=True),
            lax.all_gather(packet[1], ("pool", "batch"), axis=0, tiled=True),
            lax.all_gather(packet[2], ("pool", "batch"), axis=0, tiled=True),
        ),
    )
    new_key = arrived[0].astype(bf16).reshape(stretch, local, HEAD_DIM)
    new_value = arrived[1].astype(bf16).reshape(stretch, local, HEAD_DIM)
    new_len = arrived[2]
    steps = dec_tokens.shape[0]
    rows = dec_tokens.shape[1]
    cached = cache_k.shape[1]
    cache_key = cache_k.reshape(rows, cached, local, HEAD_DIM)
    cache_value = cache_v.reshape(rows, cached, local, HEAD_DIM)
    fresh = jnp.arange(rows, dtype=jnp.int32) == slot[0, 0]
    begin = jnp.where(fresh, new_len, cache_len)
    normed_steps = rms_norm(dec_tokens, gain)
    joined_all = jnp.dot(normed_steps.reshape(steps * rows, -1), w_qkv, preferred_element_type=f32)
    joined_all = joined_all.reshape(steps, rows, local, GROUP + 2, HEAD_DIM)
    where_all = begin[None, :] + jnp.arange(steps, dtype=jnp.int32)[:, None]
    all_query = rotate(joined_all[:, :, :, :GROUP], where_all[:, :, None, None]).astype(bf16)
    all_key = rotate(joined_all[:, :, :, GROUP], where_all[:, :, None]).astype(bf16)
    all_value = joined_all[:, :, :, GROUP + 1].astype(bf16)
    own_mask = jnp.arange(steps)[None, :] <= jnp.arange(steps)[:, None]
    attended = attend(
        all_query,
        cache_key,
        cache_value,
        cache_len,
        fresh,
        new_key,
        new_value,
        new_len,
        all_key,
        all_value,
        own_mask,
    )
    partial_value = jnp.dot(
        attended.reshape(steps * rows, local * GROUP * HEAD_DIM), w_out, preferred_element_type=f32
    )
    total = lax.psum(partial_value.reshape(steps, rows, -1).astype(jnp.bfloat16), "blk").astype(
        jnp.float32
    )
    dec_out = (dec_tokens.astype(f32) + total).astype(bf16)
    return (prefill_out, dec_out)


def solution(mesh):
    return jax.shard_map(
        body,
        mesh=mesh,
        in_specs=(
            P(("pool", "batch"), "blk", None),
            P("pool", "batch"),
            P(None, ("pool", "batch"), None),
            P(("pool", "batch"), None, "blk"),
            P(("pool", "batch"), None, "blk"),
            P(("pool", "batch")),
            P("pool", "batch"),
            P("pool", "batch"),
            P(),
            P(None, "blk"),
            P("blk", None),
        ),
        out_specs=(P(("pool", "batch"), "blk", None), P(None, ("pool", "batch"), None)),
        check_vma=False,
    )
```

profile of v0, /device:TPU:0, one launch (start us, length us, event | category | flops | bytes accessed | tf_op | source)
XLA Modules:
  0.0 270.2 jit_solution(3102997159037806648)
XLA Ops:
  7.2 1.5 fusion.25
  8.8 2.5 fusion.27
  13.3 13.0 %all-reduce = s32[8]{0:T(128)S(1)} all-reduce(s32[8]{0:T(128)S(1)} %bitcast_dynamic-update-slice_fusion), channel_id=2, replica_groups=mesh['pool'=2,'blk'=4,'batch'=4] {'pool','batch'}, use_global_device_ids=true, to_apply=%add | all-reduce | flops 8 | bytes 64 | tf_op jit(solution)/shard_map/all_gather | solution.py:142
  27.6 16.9 %copy.77 = bf16[4096,1536]{0,1:T(8,128)(2,1)} copy(bf16[4096,1536]{1,0:T(8,128)(2,1)} %param.20) | data formatting | bytes 25165824 | tf_op args[9]
  47.1 6.6 %fusion.56 = f32[4,4,2,6,128]{4,1,3,2,0:T(4,128)S(1)} fusion(bf16[2,6,128,4096,1]{3,2,1,0,4:T(8,128)(2,1)} %bitcast.123, bf16[4,4,4096]{2,1,0:T(4,128)(2,1)S(1)} %copy-done.6, f32[4096]{0:T(1024)S(1)} %copy-done.11, f32[4,4]{1,0:T(4,128)S(1)} %add_rsqrt_fusion), kind=kOutput, calls=%fused_computation.73 | convolution fusion | flops 201588736 | bytes 12828736 | tf_op jit(solution)/shard_map/dot_general | solution.py:156
  53.7 10.7 %fusion.79 = f32[512,1536]{0,1:T(8,128)S(1)} fusion(bf16[512,4096]{1,0:T(8,128)(2,1)} %all-gather.5.cloned.1.call-done, bf16[4096,1536]{1,0:T(8,128)(2,1)} %param.20), kind=kOutput, calls=%fused_computation.120 | convolution fusion | flops 6442450944 | bytes 19922944 | tf_op jit(solution)/shard_map/dot_general | solution.py:100
  64.4 1.6 copy-done.1
  74.8 12.5 %reshape.382 = bf16[4,4096,2,128]{3,2,1,0:T(2,128)(2,1)} reshape(bf16[4,4096,256]{2,1,0:T(8,128)(2,1)} %param.14) | data formatting | bytes 16777216 | tf_op jit(solution)/shard_map/reshape | solution.py:151
  87.3 12.7 %reshape.383 = bf16[4,4096,2,128]{3,2,1,0:T(2,128)(2,1)} reshape(bf16[4,4096,256]{2,1,0:T(8,128)(2,1)} %param.15) | data formatting | bytes 16777216 | tf_op jit(solution)/shard_map/reshape | solution.py:152
  100.1 6.5 %fusion.76 = (f32[4,4,2,4]{3,0,2,1:T(4,128)}, f32[4,4,2,4,4096]{4,3,0,2,1:T(4,128)S(1)}) fusion(bf16[4,4096,2,128,1]{3,2,1,0,4:T(2,128)(2,1)} %bitcast.125, bf16[4,4,2,4,128]{4,1,3,2,0:T(4,128)(2,1)S(1)} %pad_maximum_fusion, pred[4,4096]{1,0:T(4,128)(4,1)S(1)} %fusion.61), kind=kOutput, calls=%fused_computation.118 | convolution fusion | flops 135790464 | bytes 10535424 | tf_op jit(solution)/shard_map/srhgd,rchd->srhgc/dot_general | solution.py:61
  107.8 3.2 %copy.122 = f32[512,2,4,64]{3,0,2,1:T(8,128)} copy(f32[512,2,4,64]{0,3,2,1:T(8,128)} %get-tuple-element.7) | data formatting | bytes 2097152
  110.9 2.0 copy.123
  112.9 2.8 %subtract_convert_fusion = (bf16[512,2,4,64]{3,0,2,1:T(8,128)(2,1)S(1)}, bf16[512,2,4,64]{3,0,2,1:T(8,128)(2,1)S(1)}) fusion(f32[512,2,4,64]{3,0,2,1:T(8,128)} %copy.123, f32[512,2,4,64]{3,0,2,1:T(8,128)} %copy.122, f32[512,64]{1,0:T(8,128)} %copy-done.3, f32[512,64]{1,0:T(8,128)S(1)} %get-tuple-element.16), kind=kLoop, calls=%fused_computation.33 | loop fusion | flops 2097152 | bytes 3407872 | tf_op jit(solution)/shard_map/convert.6
  117.1 5.5 %fusion.74 = (f32[2,4,512]{2,1,0:T(4,128)S(1)}, f32[2,4,512,512]{2,3,1,0:T(8,128)}) fusion(f32[2,512,512,4]{2,1,3,0:T(8,128)S(1)} %fusion.42, pred[512,512]{0,1:T(8,128)(4,1)S(1)} %copy-done.8), kind=kOutput, calls=%fused_computation.116 | output fusion | flops 12583423 | bytes 17055744 | tf_op jit(solution)/shard_map/sub | solution.py:33
  122.6 5.5 %fusion.29 = bf16[2,128,4,512]{3,1,2,0:T(8,128)(2,1)} fusion(f32[2,4,512,512]{2,3,1,0:T(8,128)} %get-tuple-element.19, f32[2,4,512]{2,1,0:T(4,128)S(1)} %get-tuple-element.18, f32[512,2,6,128]{0,3,2,1:T(8,128)} %bitcast.129), kind=kOutput, calls=%fused_computation.34 | convolution fusion | flops 541589504 | bytes 9715712 | tf_op jit(solution)/shard_map/hgqk,khd->qhgd/dot_general | solution.py:114
  128.1 36.8 %all-gather.9.cloned.1.call-done = bf16[8,512,256]{2,1,0:T(8,128)(2,1)} async-done(((bf16[1,512,256]{2,1,0:T(8,128)(2,1)}), bf16[8,512,256]{2,1,0:T(8,128)(2,1)}) %all-gather.9.cloned.1.call-update) | async-done | bytes 2097168 | tf_op jit(solution)/shard_map/all_gather | solution.py:141
  165.0 3.9 %select_reduce_fusion = (bf16[512,256]{1,0:T(8,128)(2,1)}, bf16[512,256]{1,0:T(8,128)(2,1)S(1)}) fusion(bf16[8,512,256]{2,1,0:T(8,128)(2,1)} %all-gather.9.cloned.1.call-done, pred[8]{0:T(512)(128)(4,1)S(1)} %copy-done.16, bf16[8,512,256]{2,1,0:T(8,128)(2,1)} %all-gather.7.cloned.1.call-done), kind=kLoop, calls=%fused_computation.16 | loop fusion | flops 6029312 | bytes 4718600 | tf_op jit(solution)/shard_map/reduce_sum | solution.py:41
  173.1 4.7 %fusion.32 = f32[4,4,2,4,128]{4,3,0,2,1:T(4,128)S(1)} fusion(bf16[4,4096,2,128,1]{3,2,1,0,4:T(2,128)(2,1)} %bitcast.124, bf16[4,4,2,4,4612]{4,3,0,2,1:T(4,128)(2,1)S(1)} %divide_convert_fusion.2), kind=kOutput, calls=%fused_computation.38 | convolution fusion | flops 134217728 | bytes 9502720 | tf_op jit(solution)/shard_map/srhgc,rchd->srhgd/dot_general | solution.py:74
  178.3 5.4 %fusion.11 = bf16[4,4,4096]{2,1,0:T(4,128)(2,1)} fusion(bf16[4,4,1024]{2,1,0:T(4,128)(2,1)S(1)} %dot_general.55, bf16[1024,4096]{1,0:T(8,128)(2,1)} %param.21), kind=kOutput, calls=%fused_computation.13 | convolution fusion | flops 134283264 | bytes 8552448 | tf_op jit(solution)/shard_map/dot_general | solution.py:176
  183.8 9.5 %convolution_convert_fusion = bf16[512,4096]{1,0:T(8,128)(2,1)} fusion(bf16[512,1024]{0,1:T(8,128)(2,1)S(1)} %bitcast.140, bf16[1024,4096]{1,0:T(8,128)(2,1)} %param.21), kind=kOutput, calls=%fused_computation.11 | convolution fusion | flops 4297064448 | bytes 13631488 | tf_op jit(solution)/shard_map/dot_general | solution.py:118
  193.3 20.9 %all-reduce.3.cloned.1.call-done = bf16[4,4,4096]{2,1,0:T(4,128)(2,1)} async-done(((bf16[4,4,4096]{2,1,0:T(4,128)(2,1)}), bf16[4,4,4096]{2,1,0:T(4,128)(2,1)}) %all-reduce.3.cloned.1.call-update) | async-done | bytes 131088 | tf_op jit(solution)/shard_map/psum | solution.py:179
  214.2 1.6 fusion.52
  215.8 45.4 %reduce-scatter.2.cloned.1.call-done = bf16[128,4096]{1,0:T(8,128)(2,1)} async-done(((bf16[512,4096]{1,0:T(8,128)(2,1)}), bf16[128,4096]{1,0:T(8,128)(2,1)}) %reduce-scatter.2.cloned.1.call-update) | async-done | bytes 1048592 | tf_op jit(solution)/shard_map/reduce_scatter | solution.py:117
  261.2 2.4 fusion.40
  (98 shorter events, 19.7 us)
Async XLA Ops:
  7.2 4.8 %copy-start.18 = (u32[32]{0:T(128)S(1)}, u32[32]{0:T(128)}, u32[]{:S(2)}) copy-start(u32[32]{0:T(128)} %constant.44) | copy-start | bytes 388
  7.2 46.5 %all-gather.5.cloned.1.call-start = ((), (), s32[]{:S(2)}) async-start(), calls=%async_computation.1 | async-start | bytes 5242880 | tf_op jit(solution)/shard_map/all_gather | solution.py:101
  11.3 116.8 %all-gather.7.cloned.1.call-start = ((), (), s32[]{:S(2)}) async-start(), calls=%async_computation.3 | async-start | bytes 2359296 | tf_op jit(solution)/shard_map/all_gather | solution.py:140
  27.6 18.3 %copy-start.6 = (bf16[4,4,4096]{2,1,0:T(4,128)(2,1)S(1)}, bf16[4,4,4096]{2,1,0:T(4,128)(2,1)}, u32[]{:S(2)}) copy-start(bf16[4,4,4096]{2,1,0:T(4,128)(2,1)} %param.13) | copy-start | bytes 393220
  27.6 19.4 %copy-start.11 = (f32[4096]{0:T(1024)S(1)}, f32[4096]{0:T(1024)}, u32[]{:S(2)}) copy-start(f32[4096]{0:T(1024)} %param.19) | copy-start | bytes 49156
  47.1 19.2 %copy-start.3 = (f32[512,64]{1,0:T(8,128)}, f32[512,64]{1,0:T(8,128)S(1)}, u32[]{:S(2)}) copy-start(f32[512,64]{1,0:T(8,128)S(1)} %get-tuple-element.17) | copy-start | bytes 393220
  64.4 1.6 copy-start.1
  66.0 1.8 copy-start.15
  66.7 20.6 %copy-start.4 = (bf16[512,2,128]{2,0,1:T(8,128)(2,1)}, bf16[512,2,128]{2,0,1:T(8,128)(2,1)S(1)}, u32[]{:S(2)}) copy-start(bf16[512,2,128]{2,0,1:T(8,128)(2,1)S(1)} %maximum_convert_fusion) | copy-start | bytes 786436
  67.7 97.2 %all-gather.9.cloned.1.call-start = ((), (), s32[]{:S(2)}) async-start(), calls=%async_computation.4 | async-start | bytes 2359296 | tf_op jit(solution)/shard_map/all_gather | solution.py:141
  69.0 31.1 %copy-start.9 = (bf16[4,4,2,4,128]{4,1,3,2,0:T(4,128)(2,1)}, bf16[4,4,2,4,128]{4,1,3,2,0:T(4,128)(2,1)S(1)}, u32[]{:S(2)}) copy-start(bf16[4,4,2,4,128]{4,1,3,2,0:T(4,128)(2,1)S(1)} %pad_maximum_fusion) | copy-start | bytes 98308
  74.0 140.2 %all-reduce.3.cloned.1.call-start = ((), (), s32[]{:S(2)}) async-start(), calls=%async_computation.5 | async-start | bytes 262144 | tf_op jit(solution)/shard_map/psum | solution.py:179
  100.1 6.5 %copy-start.2 = (f32[512,1536]{0,1:T(8,128)S(1)}, f32[512,1536]{0,1:T(8,128)}, u32[]{:S(2)}) copy-start(f32[512,1536]{0,1:T(8,128)} %copy-done.1) | copy-start | bytes 9437188
  112.9 2.9 %copy-start.5 = (bf16[512,2,128]{2,0,1:T(8,128)(2,1)S(1)}, bf16[512,2,128]{2,0,1:T(8,128)(2,1)}, u32[]{:S(2)}) copy-start(bf16[512,2,128]{2,0,1:T(8,128)(2,1)} %copy-done.4) | copy-start | bytes 786436
  115.8 1.4 copy-start.8
  122.6 42.3 %copy-start.16 = (pred[8]{0:T(512)(128)(4,1)S(1)}, pred[8]{0:T(512)(128)(4,1)}, u32[]{:S(2)}) copy-start(pred[8]{0:T(512)(128)(4,1)} %iota_compare_fusion.5) | copy-start | bytes 28
  128.1 40.9 %copy-start.10 = (bf16[4,4,2,4,128]{4,1,3,2,0:T(4,128)(2,1)S(1)}, bf16[4,4,2,4,128]{4,1,3,2,0:T(4,128)(2,1)}, u32[]{:S(2)}) copy-start(bf16[4,4,2,4,128]{4,1,3,2,0:T(4,128)(2,1)} %copy-done.9) | copy-start | bytes 98308
  128.1 40.9 %copy-start.14 = (pred[4,512]{1,0:T(4,128)(4,1)S(1)}, pred[4,512]{1,0:T(4,128)(4,1)}, u32[]{:S(2)}) copy-start(pred[4,512]{1,0:T(4,128)(4,1)} %broadcast_and_fusion) | copy-start | bytes 6148
  128.1 41.3 %copy-start.12 = (f32[4,4,2,4]{3,0,2,1:T(4,128)S(1)}, f32[4,4,2,4]{3,0,2,1:T(4,128)}, u32[]{:S(2)}) copy-start(f32[4,4,2,4]{3,0,2,1:T(4,128)} %get-tuple-element.22) | copy-start | bytes 1540
  128.1 41.3 %copy-start.7 = (f32[4,4,2,4,4]{4,3,0,2,1:T(4,128)S(1)}, f32[4,4,2,4,4]{4,3,0,2,1:T(4,128)}, u32[]{:S(2)}) copy-start(f32[4,4,2,4,4]{4,3,0,2,1:T(4,128)} %get-tuple-element.21) | copy-start | bytes 6148
  173.1 5.0 %copy-start.13 = (bf16[4,4,2,128,1]{3,1,2,0,4:T(4,128)(2,1)S(1)}, bf16[4,4,2,128,1]{3,1,2,0,4:T(4,128)(2,1)}, u32[]{:S(2)}) copy-start(bf16[4,4,2,128,1]{3,1,2,0,4:T(4,128)(2,1)} %fusion.66) | copy-start | bytes 24580
  178.3 5.5 %copy-start.17 = (bf16[2,128,4,512]{3,1,2,0:T(8,128)(2,1)S(1)}, bf16[2,128,4,512]{3,1,2,0:T(8,128)(2,1)}, u32[]{:S(2)}) copy-start(bf16[2,128,4,512]{3,1,2,0:T(8,128)(2,1)} %fusion.29) | copy-start | bytes 3145732
  183.7 77.5 %reduce-scatter.2.cloned.1.call-start = ((), (), s32[]{:S(2)}) async-start(), calls=%async_computation.2 | async-start | bytes 5242880 | tf_op jit(solution)/shard_map/reduce_scatter | solution.py:117
  193.3 67.9 %copy-start = (bf16[1,128,4096]{2,1,0:T(8,128)(2,1)S(1)}, bf16[1,128,4096]{2,1,0:T(8,128)(2,1)}, u32[]{:S(2)}) copy-start(bf16[1,128,4096]{2,1,0:T(8,128)(2,1)} %param.11) | copy-start | bytes 3145732
Sparse Core Ops, SparseCore 0:
  11.4 37.1 all-gather.4
  67.8 47.2 all-gather.6
  117.3 47.6 all-gather.8
  183.8 30.3 all-reduce.2
  216.5 44.5 reduce-scatter.1
where the time goes:
time: 272 us; the launch traced here: 270 us
  waiting for transfers between devices  103 us (38%)
  local copies, waits for them, and re-layouts  56.5 us (21%)
  matrix products  51.7 us (19%)
  other arithmetic  29.2 us (11%)
  between operations  16.2 us (6%)
  blocking collectives  13 us (5%)
    reduce_scatter x1, waiting for transfers between devices, body(): lax.psum_scatter(jnp.dot(rows, w_out, preferred_element_type=f32).astype(...  45.4 us
    all_gather x1, waiting for transfers between devices, body(): lax.all_gather(packet[1], ('pool', 'batch'), axis=0, tiled=True)  36.8 us
    unnamed x45, local copies, waits for them, and re-layouts  25.2 us
    psum x1, waiting for transfers between devices, body(): lax.psum(partial_value.reshape(steps, rows, -1).astype(jnp.bfloat16), 'blk')  20.9 us
    all_gather x1, blocking collectives, body(): lax.all_gather(packet[2], ('pool', 'batch'), axis=0, tiled=True)  13 us
    reshape x1, local copies, waits for them, and re-layouts, body(): cache_value = cache_v.reshape(rows, cached, local, HEAD_DIM)  12.7 us
    reshape x1, local copies, waits for them, and re-layouts, body(): cache_key = cache_k.reshape(rows, cached, local, HEAD_DIM)  12.5 us
    dot_general x1, matrix products, body(): jnp.dot(lax.all_gather(normed, 'blk', axis=0, tiled=True), w_qkv, preferr...  10.7 us
  transfers between devices with their start and end apart: 5, of which 3 were waited for; matrix products, arithmetic and copies ran while one was open for 36% of the time, Pallas kernels for 0%

commit v1 on v0

--- a/solution.py
+++ b/solution.py
@@ -176,9 +176,9 @@
     partial_value = jnp.dot(
         attended.reshape(steps * rows, local * GROUP * HEAD_DIM), w_out, preferred_element_type=f32
     )
-    total = lax.psum(partial_value.reshape(steps, rows, -1).astype(jnp.bfloat16), "blk").astype(
-        jnp.float32
-    )
+    total = jnp.sum(
+        lax.all_gather(partial_value.reshape(steps, rows, -1).astype(jnp.bfloat16), "blk"), axis=0
+    ).astype(jnp.float32)
     dec_out = (dec_tokens.astype(f32) + total).astype(bf16)
     return (prefill_out, dec_out)
 

time: 272 us -> 220 us (0.81)
  waiting for transfers between devices: 103 us -> 51 us
  blocking collectives: 13 us -> 21.7 us
  matrix products: 51.7 us -> 46.7 us
    all_gather x1, waiting for transfers between devices: 36.8 us -> 0.02 us  [body(): lax.all_gather(packet[1], ('pool', 'batch'), axis=0, tiled=True)]
    all_gather x1, waiting for transfers between devices: 0.02 us -> 34.2 us  [body(): lax.all_gather(normed, 'blk', axis=0, tiled=True)]
    reduce_scatter x1, waiting for transfers between devices: 45.4 us -> 16.7 us  [body(): lax.psum_scatter(jnp.dot(rows, w_out, preferred_element_type=f32).astype(...]
    psum x1 -> x0, waiting for transfers between devices: 20.9 us -> none  [body(): lax.psum(partial_value.reshape(steps, rows, -1).astype(jnp.bfloat16), 'blk')]
    all_gather x0 -> x1, blocking collectives: none -> 10.4 us  [body(): lax.all_gather(partial_value.reshape(steps, rows, -1).astype(jnp.bfloat16...]
    dot_general x1, matrix products: 9.5 us -> 6.27 us  [body(): jnp.dot(rows, w_out, preferred_element_type=f32).astype(jnp.bfloat16)]
    unnamed x45 -> x41, local copies, waits for them, and re-layouts: 25.2 us -> 24.2 us
  transfers between devices with their start and end apart: 5 -> 4, of which waited for: 3 -> 2; matrix products, arithmetic and copies ran while one was open for 36% -> 50% of each run, Pallas kernels for 0% -> 0%
where the time goes in v1:
time: 220 us; the launch traced here: 219 us
  local copies, waits for them, and re-layouts  55.4 us (25%)
  waiting for transfers between devices  51 us (23%)
  matrix products  46.7 us (21%)
  other arithmetic  27.7 us (13%)
  blocking collectives  21.7 us (10%)
  between operations  16.1 us (7%)
    all_gather x1, waiting for transfers between devices, body(): lax.all_gather(normed, 'blk', axis=0, tiled=True)  34.2 us
    unnamed x41, local copies, waits for them, and re-layouts  24.2 us
    reduce_scatter x1, waiting for transfers between devices, body(): lax.psum_scatter(jnp.dot(rows, w_out, preferred_element_type=f32).astype(...  16.7 us
    reshape x1, local copies, waits for them, and re-layouts, body(): cache_key = cache_k.reshape(rows, cached, local, HEAD_DIM)  12.6 us
    reshape x1, local copies, waits for them, and re-layouts, body(): cache_value = cache_v.reshape(rows, cached, local, HEAD_DIM)  12.6 us
    all_gather x1, blocking collectives, body(): lax.all_gather(packet[2], ('pool', 'batch'), axis=0, tiled=True)  11.3 us
    dot_general x1, matrix products, body(): jnp.dot(lax.all_gather(normed, 'blk', axis=0, tiled=True), w_qkv, preferr...  10.6 us
    all_gather x1, blocking collectives, body(): lax.all_gather(partial_value.reshape(steps, rows, -1).astype(jnp.bfloat16...  10.4 us
  transfers between devices with their start and end apart: 4, of which 2 were waited for; matrix products, arithmetic and copies ran while one was open for 50% of the time, Pallas kernels for 0%

profile of v1, /device:TPU:0, one launch (start us, length us, event | category | flops | bytes accessed | tf_op | source)
XLA Modules:
  0.0 219.0 jit_solution(1300038439614414521)
XLA Ops:
  7.2 1.5 fusion.25
  8.8 2.5 %fusion.27 = bf16[128,4096]{1,0:T(8,128)(2,1)} fusion(bf16[1,128,4096]{2,1,0:T(8,128)(2,1)} %param.11, f32[4096]{0:T(1024)} %param.19, f32[128]{0:T(128)S(1)} %add_rsqrt_fusion.1), kind=kLoop, calls=%fused_computation.30 | loop fusion | flops 2097152 | bytes 2114048 | tf_op jit(solution)/shard_map/convert_element_type | solution.py:15
  14.4 34.2 %all-gather.6.cloned.1.call-done = bf16[512,4096]{1,0:T(8,128)(2,1)} async-done(((bf16[128,4096]{1,0:T(8,128)(2,1)}), bf16[512,4096]{1,0:T(8,128)(2,1)}) %all-gather.6.cloned.1.call-update) | async-done | bytes 4194320 | tf_op jit(solution)/shard_map/all_gather | solution.py:101
  48.6 10.6 %fusion.79 = f32[512,1536]{0,1:T(8,128)S(1)} fusion(bf16[512,4096]{1,0:T(8,128)(2,1)} %all-gather.6.cloned.1.call-done, bf16[4096,1536]{1,0:T(8,128)(2,1)} %param.20), kind=kOutput, calls=%fused_computation.120 | convolution fusion | flops 6442450944 | bytes 19922944 | tf_op jit(solution)/shard_map/dot_general | solution.py:100
  59.3 1.7 copy-done.1
  63.3 11.3 %all-reduce = s32[8]{0:T(128)S(1)} all-reduce(s32[8]{0:T(128)S(1)} %bitcast_dynamic-update-slice_fusion), channel_id=2, replica_groups=mesh['pool'=2,'blk'=4,'batch'=4] {'pool','batch'}, use_global_device_ids=true, to_apply=%add | all-reduce | flops 8 | bytes 64 | tf_op jit(solution)/shard_map/all_gather | solution.py:142
  74.6 16.9 %copy.77 = bf16[4096,1536]{0,1:T(8,128)(2,1)} copy(bf16[4096,1536]{1,0:T(8,128)(2,1)} %param.20) | data formatting | bytes 25165824 | tf_op args[9]
  97.0 7.1 %fusion.56 = f32[4,4,2,6,128]{4,1,3,2,0:T(4,128)} fusion(bf16[2,6,128,4096,1]{3,2,1,0,4:T(8,128)(2,1)} %bitcast.124, bf16[4,4,4096]{2,1,0:T(4,128)(2,1)S(1)} %copy-done.5, f32[4096]{0:T(1024)S(1)} %copy-done.8, f32[4,4]{1,0:T(4,128)S(1)} %add_rsqrt_fusion), kind=kOutput, calls=%fused_computation.73 | convolution fusion | flops 201588736 | bytes 12828736 | tf_op jit(solution)/shard_map/dot_general | solution.py:156
  106.1 2.8 %fusion.73 = (f32[512,2,4,64]{0,3,2,1:T(8,128)S(1)}, f32[512,2,4,64]{0,3,2,1:T(8,128)}) fusion(f32[512,2,6,128]{0,3,2,1:T(8,128)} %bitcast.132), kind=kLoop, calls=%fused_computation.115 | loop fusion | bytes 4194304 | tf_op jit(solution)/shard_map/slice | solution.py:25
  108.8 1.8 copy.122
  110.7 1.9 copy.123
  112.8 2.1 subtract_convert_fusion
  116.4 5.6 %fusion.74 = (f32[2,4,512]{2,1,0:T(4,128)S(1)}, f32[2,4,512,512]{2,3,1,0:T(8,128)}) fusion(f32[2,512,512,4]{2,1,3,0:T(8,128)S(1)} %fusion.42, pred[512,512]{0,1:T(8,128)(4,1)S(1)} %copy-done.6), kind=kOutput, calls=%fused_computation.116 | output fusion | flops 12583423 | bytes 17055744 | tf_op jit(solution)/shard_map/sub | solution.py:33
  122.0 4.4 %fusion.29 = bf16[2,128,4,512]{3,1,2,0:T(8,128)(2,1)S(1)} fusion(f32[2,4,512,512]{2,3,1,0:T(8,128)} %get-tuple-element.19, f32[2,4,512]{2,1,0:T(4,128)S(1)} %get-tuple-element.18, f32[512,2,6,128]{0,3,2,1:T(8,128)} %bitcast.133), kind=kOutput, calls=%fused_computation.34 | convolution fusion | flops 541589504 | bytes 9715712 | tf_op jit(solution)/shard_map/hgqk,khd->qhgd/dot_general | solution.py:114
  126.7 6.3 %convolution_convert_fusion = bf16[512,4096]{1,0:T(8,128)(2,1)} fusion(bf16[512,1024]{0,1:T(8,128)(2,1)S(1)} %bitcast.144, bf16[1024,4096]{1,0:T(8,128)(2,1)S(1)} %bitcast.126), kind=kOutput, calls=%fused_computation.11 | convolution fusion | flops 4297064448 | bytes 13631488 | tf_op jit(solution)/shard_map/dot_general | solution.py:118
  133.0 12.6 %reshape.382 = bf16[4,4096,2,128]{3,2,1,0:T(2,128)(2,1)} reshape(bf16[4,4096,256]{2,1,0:T(8,128)(2,1)} %param.14) | data formatting | bytes 16777216 | tf_op jit(solution)/shard_map/reshape | solution.py:151
  145.6 12.6 %reshape.383 = bf16[4,4096,2,128]{3,2,1,0:T(2,128)(2,1)} reshape(bf16[4,4096,256]{2,1,0:T(8,128)(2,1)} %param.15) | data formatting | bytes 16777216 | tf_op jit(solution)/shard_map/reshape | solution.py:152
  159.1 5.8 %fusion.76 = (f32[4,4,2,4]{3,0,2,1:T(4,128)S(1)}, f32[4,4,2,4,4096]{4,3,0,2,1:T(4,128)S(1)}) fusion(bf16[4,4096,2,128,1]{3,2,1,0,4:T(2,128)(2,1)} %bitcast.128, bf16[4,4,2,4,128]{4,1,3,2,0:T(4,128)(2,1)S(1)} %pad_maximum_fusion, pred[4,4096]{1,0:T(4,128)(4,1)S(1)} %fusion.61), kind=kOutput, calls=%fused_computation.118 | convolution fusion | flops 135790464 | bytes 10535424 | tf_op jit(solution)/shard_map/srhgd,rchd->srhgc/dot_general | solution.py:61
  164.9 3.1 %select_reduce_fusion = (bf16[512,256]{1,0:T(8,128)(2,1)S(1)}, bf16[512,256]{1,0:T(8,128)(2,1)S(1)}) fusion(bf16[8,512,256]{2,1,0:T(8,128)(2,1)} %all-gather.10.cloned.1.call-done, pred[8]{0:T(512)(128)(4,1)S(1)} %copy-done.11, bf16[8,512,256]{2,1,0:T(8,128)(2,1)} %all-gather.8.cloned.1.call-done), kind=kLoop, calls=%fused_computation.16 | loop fusion | flops 6029312 | bytes 4718600 | tf_op jit(solution)/shard_map/reduce_sum | solution.py:41
  171.2 5.5 %fusion.32 = f32[4,4,2,4,128]{4,3,0,2,1:T(4,128)S(1)} fusion(bf16[4,4096,2,128,1]{3,2,1,0,4:T(2,128)(2,1)} %bitcast.127, bf16[4,4,2,4,4612]{4,3,0,2,1:T(4,128)(2,1)S(1)} %divide_convert_fusion.2), kind=kOutput, calls=%fused_computation.38 | convolution fusion | flops 134217728 | bytes 9502720 | tf_op jit(solution)/shard_map/srhgc,rchd->srhgd/dot_general | solution.py:74
  177.2 4.7 %fusion.11 = bf16[4,4,4096]{2,1,0:T(4,128)(2,1)S(1)} fusion(bf16[4,4,1024]{2,1,0:T(4,128)(2,1)S(1)} %dot_general.55, bf16[1024,4096]{1,0:T(8,128)(2,1)} %param.21), kind=kOutput, calls=%fused_computation.13 | convolution fusion | flops 134283264 | bytes 8552448 | tf_op jit(solution)/shard_map/dot_general | solution.py:176
  181.9 10.4 %all-gather.1 = bf16[16,4,4096]{2,1,0:T(4,128)(2,1)S(1)} all-gather(bf16[4,4,4096]{2,1,0:T(4,128)(2,1)S(1)} %fusion.11), channel_id=3, replica_groups=mesh['pool'=2,'blk'=4,'batch'=4] {'blk'}, dimensions={0}, use_global_device_ids=true | all-gather | bytes 655360 | tf_op jit(solution)/shard_map/all_gather | solution.py:180
  193.3 16.7 %reduce-scatter.2.cloned.1.call-done = bf16[128,4096]{1,0:T(8,128)(2,1)} async-done(((bf16[512,4096]{1,0:T(8,128)(2,1)}), bf16[128,4096]{1,0:T(8,128)(2,1)}) %reduce-scatter.2.cloned.1.call-update) | async-done | bytes 1048592 | tf_op jit(solution)/shard_map/reduce_scatter | solution.py:117
  210.0 2.4 %fusion.40 = bf16[1,128,4096]{2,1,0:T(8,128)(2,1)} fusion(bf16[128,4096]{1,0:T(8,128)(2,1)} %reduce-scatter.2.cloned.1.call-done, bf16[1,128,4096]{2,1,0:T(8,128)(2,1)S(1)} %copy-done), kind=kLoop, calls=%fused_computation.47 | loop fusion | flops 2097152 | bytes 3145728 | tf_op jit(solution)/shard_map/broadcast_in_dim | solution.py:123
  (94 shorter events, 18.3 us)
Async XLA Ops:
  7.2 4.8 %copy-start.13 = (u32[32]{0:T(128)S(1)}, u32[32]{0:T(128)}, u32[]{:S(2)}) copy-start(u32[32]{0:T(128)} %constant.46) | copy-start | bytes 388
  7.2 41.5 %all-gather.6.cloned.1.call-start = ((), (), s32[]{:S(2)}) async-start(), calls=%async_computation.1 | async-start | bytes 5242880 | tf_op jit(solution)/shard_map/all_gather | solution.py:101
  11.3 153.6 %all-gather.8.cloned.1.call-start = ((), (), s32[]{:S(2)}) async-start(), calls=%async_computation.3 | async-start | bytes 2359296 | tf_op jit(solution)/shard_map/all_gather | solution.py:140
  14.4 46.8 %copy-start.2 = (f32[512,64]{1,0:T(8,128)}, f32[512,64]{1,0:T(8,128)S(1)}, u32[]{:S(2)}) copy-start(f32[512,64]{1,0:T(8,128)S(1)} %get-tuple-element.17) | copy-start | bytes 393220
  59.3 1.7 copy-start.1
  61.6 29.9 %copy-start.3 = (bf16[512,2,128]{2,0,1:T(8,128)(2,1)}, bf16[512,2,128]{2,0,1:T(8,128)(2,1)S(1)}, u32[]{:S(2)}) copy-start(bf16[512,2,128]{2,0,1:T(8,128)(2,1)S(1)} %maximum_convert_fusion) | copy-start | bytes 786436
  62.6 102.3 %all-gather.10.cloned.1.call-start = ((), (), s32[]{:S(2)}) async-start(), calls=%async_computation.4 | async-start | bytes 2359296 | tf_op jit(solution)/shard_map/all_gather | solution.py:141
  74.6 20.6 %copy-start.5 = (bf16[4,4,4096]{2,1,0:T(4,128)(2,1)S(1)}, bf16[4,4,4096]{2,1,0:T(4,128)(2,1)}, u32[]{:S(2)}) copy-start(bf16[4,4,4096]{2,1,0:T(4,128)(2,1)} %param.13) | copy-start | bytes 393220
  74.6 20.7 %copy-start.9 = (s32[4]{0:T(128)S(1)}, s32[4]{0:T(128)}, u32[]{:S(2)}) copy-start(s32[4]{0:T(128)} %param.16) | copy-start | bytes 52
  74.6 22.4 %copy-start.8 = (f32[4096]{0:T(1024)S(1)}, f32[4096]{0:T(1024)}, u32[]{:S(2)}) copy-start(f32[4096]{0:T(1024)} %param.19) | copy-start | bytes 49156
  112.6 2.4 %copy-start.4 = (bf16[512,2,128]{2,0,1:T(8,128)(2,1)S(1)}, bf16[512,2,128]{2,0,1:T(8,128)(2,1)}, u32[]{:S(2)}) copy-start(bf16[512,2,128]{2,0,1:T(8,128)(2,1)} %copy-done.3) | copy-start | bytes 786436
  112.6 97.4 %reduce-scatter.2.cloned.1.call-start = ((), (), s32[]{:S(2)}) async-start(), calls=%async_computation.2 | async-start | bytes 5242880 | tf_op jit(solution)/shard_map/reduce_scatter | solution.py:117
  115.0 1.4 copy-start.6
  116.4 10.0 %slice-start = ((s8[8388608]{0:T(1024)(128)(4,1)}), s8[4194304]{0:T(1024)(128)(4,1)S(1)}, s32[]{:S(2)}) async-start(s8[8388608]{0:T(1024)(128)(4,1)} %bitcast.125), calls=%async_computation.5 | async-start | bytes 8388608
  122.0 4.7 %slice-start.1 = ((s8[8388608]{0:T(1024)(128)(4,1)}), s8[4194304]{0:T(1024)(128)(4,1)S(1)}, s32[]{:S(2)}) async-start(s8[8388608]{0:T(1024)(128)(4,1)} %bitcast.125), calls=%async_computation.6 | async-start | bytes 8388608
  145.6 12.6 %copy-start.7 = (f32[4,4,2,6,128]{4,1,3,2,0:T(4,128)S(1)}, f32[4,4,2,6,128]{4,1,3,2,0:T(4,128)}, u32[]{:S(2)}) copy-start(f32[4,4,2,6,128]{4,1,3,2,0:T(4,128)} %fusion.56) | copy-start | bytes 294916
  145.6 13.0 %copy-start.12 = (pred[512]{0:T(512)(128)(4,1)S(1)}, pred[512]{0:T(512)(128)(4,1)}, u32[]{:S(2)}) copy-start(pred[512]{0:T(512)(128)(4,1)} %iota_compare_fusion.3) | copy-start | bytes 1540
  145.6 13.1 %copy-start.14 = (pred[4,4]{1,0:T(4,128)(4,1)S(1)}, pred[4,4]{1,0:T(4,128)(4,1)}, u32[]{:S(2)}) copy-start(pred[4,4]{1,0:T(4,128)(4,1)} %iota_compare_fusion.2) | copy-start | bytes 52
  145.6 13.3 %copy-start.10 = (s32[4]{0:T(128)S(1)}, s32[4]{0:T(128)}, u32[]{:S(2)}) copy-start(s32[4]{0:T(128)} %param.16) | copy-start | bytes 52
  159.1 5.8 %copy-start.11 = (pred[8]{0:T(512)(128)(4,1)S(1)}, pred[8]{0:T(512)(128)(4,1)}, u32[]{:S(2)}) copy-start(pred[8]{0:T(512)(128)(4,1)} %iota_compare_fusion.5) | copy-start | bytes 28
  177.1 32.8 %copy-start = (bf16[1,128,4096]{2,1,0:T(8,128)(2,1)S(1)}, bf16[1,128,4096]{2,1,0:T(8,128)(2,1)}, u32[]{:S(2)}) copy-start(bf16[1,128,4096]{2,1,0:T(8,128)(2,1)} %param.11) | copy-start | bytes 3145732
Sparse Core Ops, SparseCore 0:
  11.4 37.1 all-gather.5
  62.8 49.0 all-gather.7
  114.0 47.6 all-gather.9
  164.0 45.9 reduce-scatter.1
